TPU v7x, 128 devices: a whole 4x4x4 slice. The times are simulated.
128 devices in a mesh: seq: 16 (over z_hi, y, core), head: 8 (over x, z_lo).
Axes of the slice: x: 4, y: 4, z: 4 (z_hi: 2, z_lo: 2; z = z_hi * 2 + z_lo), core: 2. Of those that a mesh axis runs over, the one named last changes fastest.
Arguments:
- latent: bfloat16 [16, 1024, 2048], P('seq', None, 'head'), may hold values from -6 to 6
- modulation: float32 [9, 2048], replicated, may hold values from -3 to 3
- spatial_qkv: bfloat16 [3, 2048, 2048], P(None, None, 'head')
- spatial_out: bfloat16 [2048, 2048], P('head'), may hold values from -0.125 to 0.125
- temporal_qkv: bfloat16 [3, 2048, 2048], P(None, None, 'head')
- temporal_out: bfloat16 [2048, 2048], P('head'), may hold values from -0.125 to 0.125
- hidden_weight: bfloat16 [2048, 8192], P(None, 'head'), may hold values from -0.125 to 0.125
- output_weight: bfloat16 [8192, 2048], P('head'), may hold values from -0.0625 to 0.0625
Outputs:
- block_out: bfloat16 [16, 1024, 2048], P(None, 'seq', 'head')
All inputs are finite; a program needn't handle non-finite values.
Results may differ from a plain program's by a relative error of at most 0.009.
Values may be sent and summed in bfloat16 or wider, within the bound.
A program may use at most 128 MiB of HBM per device.

v0:
```python
import jax
import jax.numpy as jnp
from jax import lax
from jax.sharding import PartitionSpec as P

HD = 64


def split_up(shard, dim, devices):
    lengths = shard.shape
    blocks = shard.reshape(*lengths[:dim], devices, lengths[dim] // devices, *lengths[dim + 1 :])
    return jnp.moveaxis(blocks, dim, 0)


def sum_at_owner(shard, axis, dim):
    devices = lax.axis_size(axis)
    blocks = lax.all_to_all(split_up(shard, dim, devices), axis, 0, 0, tiled=True)
    return jnp.sum(blocks.astype(jnp.float32), axis=0)


def layer_norm(values):
    average = jnp.mean(values, axis=-1, keepdims=True)
    centred = values - average
    variance = jnp.mean(centred * centred, axis=-1, keepdims=True)
    return centred * lax.rsqrt(variance + 1e-06)


def modulate(stream, modulation, offset):
    normed = layer_norm(stream.astype(jnp.float32))
    return (normed * (1.0 + modulation[offset + 1]) + modulation[offset]).astype(jnp.bfloat16)


def attend(query, keys, values):
    scores = jnp.einsum(
        "glhd,gmhd->ghlm", query, keys, preferred_element_type=jnp.float32
    ) * HD ** (-0.5)
    attn_weights = jax.nn.softmax(scores, axis=-1).astype(jnp.bfloat16)
    return jnp.einsum(
        "ghlm,gmhd->glhd", attn_weights, values, preferred_element_type=jnp.float32
    ).astype(jnp.bfloat16)


def project_three(normed, weights):
    return [
        jnp.dot(normed, weights[member], preferred_element_type=jnp.float32).astype(jnp.bfloat16)
        for member in range(3)
    ]


def column_adder(columns, portion):
    return jnp.dot(portion, columns, preferred_element_type=jnp.float32)


def per_device(
    latent,
    modulation,
    spatial_qkv,
    spatial_out,
    temporal_qkv,
    temporal_out,
    hidden_weight,
    output_weight,
):
    width_local = latent.shape[2]
    heads_local = width_local // HD
    anchor = lax.axis_index("head") * width_local
    local_rows = lax.dynamic_slice_in_dim(modulation, anchor, width_local, 1)
    full_spatial = lax.all_gather(latent, "head", axis=2, tiled=True)
    normed = modulate(full_spatial, modulation, 0)
    frames_local = latent.shape[0]
    patches = latent.shape[1]
    query, keys, values = [
        member.reshape(frames_local, patches, heads_local, HD)
        for member in project_three(normed, spatial_qkv)
    ]
    spatial = lax.map(
        lambda triple: attend(triple[0][None], triple[1][None], triple[2][None])[0],
        (query, keys, values),
    )
    spatial = spatial.reshape(frames_local, patches, width_local)
    columns = lax.all_to_all(spatial_out, "head", split_axis=1, concat_axis=0, tiled=True)
    reduced = column_adder(columns, lax.all_gather(spatial, "head", axis=2, tiled=True))
    stream_one = (latent.astype(jnp.float32) + local_rows[2] * reduced).astype(jnp.bfloat16)
    stream_temporal = lax.all_to_all(stream_one, "seq", split_axis=1, concat_axis=0, tiled=True)
    full_temporal = lax.all_gather(stream_temporal, "head", axis=2, tiled=True)
    normed = modulate(full_temporal, modulation, 3)
    query, keys, values = project_three(normed, temporal_qkv)
    frames = stream_temporal.shape[0]
    patches_local = stream_temporal.shape[1]

    def to_groups(tensor):
        return jnp.transpose(tensor.reshape(frames, patches_local, heads_local, HD), (1, 0, 2, 3))

    temporal = attend(to_groups(query), to_groups(keys), to_groups(values))
    temporal = jnp.transpose(temporal, (1, 0, 2, 3)).reshape(frames, patches_local, width_local)
    columns = lax.all_to_all(temporal_out, "head", split_axis=1, concat_axis=0, tiled=True)
    reduced = column_adder(columns, lax.all_gather(temporal, "head", axis=2, tiled=True))
    stream_two = (stream_temporal.astype(jnp.float32) + local_rows[5] * reduced).astype(
        jnp.bfloat16
    )
    full_two = lax.all_gather(stream_two, "head", axis=2, tiled=True)
    normed = modulate(full_two, modulation, 6)
    pre_act = jnp.dot(normed, hidden_weight, preferred_element_type=jnp.float32)
    hidden = jax.nn.gelu(pre_act, approximate=True).astype(jnp.bfloat16)
    partial_sums = jnp.dot(hidden, output_weight, preferred_element_type=jnp.float32)
    reduced = sum_at_owner(partial_sums.astype(jnp.bfloat16), "head", 2)
    return (stream_two.astype(jnp.float32) + local_rows[8] * reduced).astype(jnp.bfloat16)


def solution(mesh):
    in_specs = (
        P("seq", None, "head"),
        P(),
        P(None, None, "head"),
        P("head", None),
        P(None, None, "head"),
        P("head", None),
        P(None, "head"),
        P("head", None),
    )
    out_specs = P(None, "seq", "head")
    return jax.shard_map(
        per_device, mesh=mesh, in_specs=in_specs, out_specs=out_specs, check_vma=False
    )
```

profile of v0, /device:TPU:8, one launch (start us, length us, event | category | flops | bytes accessed | tf_op | source)
XLA Modules:
  0.0 685.8 jit_solution(7628114898617417352)
XLA Ops:
  8.4 99.1 %all-gather.6.cloned.1.call-done = bf16[1,1024,2048]{2,1,0:T(8,128)(2,1)} async-done(((bf16[1,1024,256]{2,1,0:T(8,128)(2,1)}), bf16[1,1024,2048]{2,1,0:T(8,128)(2,1)}) %all-gather.6.cloned.1.call-update) | async-done | bytes 4194320 | tf_op jit(solution)/shard_map/all_gather | solution.py:68
  107.6 3.0 convert_reduce_fusion.2
  112.3 1.9 fusion.33
  114.2 1.3 convolution_convert_fusion.6
  115.5 1.3 convolution_convert_fusion.5
  118.1 5.2 fusion.130
  123.3 8.1 %fusion.136 = f32[4,1024,1024]{1,2,0:T(8,128)} fusion(bf16[1024,4,64]{0,2,1:T(8,128)(2,1)S(1)} %bitcast.142, bf16[1024,4,64]{0,2,1:T(8,128)(2,1)S(1)} %bitcast.144), kind=kOutput, calls=%fused_computation.124 | convolution fusion | flops 536870912 | bytes 17825792 | tf_op jit(solution)/shard_map/while/body/eval_jaxpr/glhd,gmhd->ghlm/dot_general | solution.py:34
  131.4 16.0 %fusion.69 = bf16[4,64,1024]{2,1,0:T(8,128)(2,1)} fusion(bf16[1024,4,64]{0,2,1:T(8,128)(2,1)S(1)} %bitcast.162, f32[4,1024]{1,0:T(4,128)S(1)} %fusion.130, f32[4,1024,1024]{1,2,0:T(8,128)} %fusion.136), kind=kOutput, calls=%fused_computation.78 | convolution fusion | flops 558109696 | bytes 17842176 | tf_op jit(solution)/shard_map/while/body/eval_jaxpr/ghlm,gmhd->glhd/dot_general | solution.py:38
  147.4 1.3 copy.43
  148.7 6.0 all-to-all-start
  155.6 21.3 %all-to-all-done = bf16[256,8,256]{0,2,1:T(8,128)(2,1)S(1)} async-done(((bf16[256,8,256]{0,2,1:T(8,128)(2,1)}), bf16[256,8,256]{0,2,1:T(8,128)(2,1)S(1)}, u32[]{:S(2)}, u32[]{:S(2)}) %all-to-all-start) | async-done | bytes 1048608 | tf_op jit(solution)/shard_map/all_to_all | solution.py:81
  177.5 71.1 %all-gather.8.cloned.1.call-done = bf16[1,1024,2048]{1,2,0:T(8,128)(2,1)} async-done(((bf16[1,1024,256]{1,2,0:T(8,128)(2,1)}), bf16[1,1024,2048]{1,2,0:T(8,128)(2,1)}) %all-gather.8.cloned.1.call-update) | async-done | bytes 4194320 | tf_op jit(solution)/shard_map/all_gather | solution.py:82
  248.6 3.5 fusion.65
  253.4 3.8 reduce.6
  257.4 15.9 %all_to_all.55 = bf16[16,2,8192]{2,1,0:T(2,128)(2,1)S(1)} all-to-all(bf16[16,2,8192]{2,1,0:T(2,128)(2,1)S(1)} %reshape.181), channel_id=1, replica_groups=mesh['seq'=16,'head'=8] {'seq'}, dimensions={0} | all-to-all | bytes 1048576 | tf_op jit(solution)/shard_map/all_to_all | solution.py:84
  274.9 94.6 %all-gather.10.cloned.1.call-done = bf16[16,64,2048]{2,1,0:T(8,128)(2,1)} async-done(((bf16[16,64,256]{2,1,0:T(8,128)(2,1)}), bf16[16,64,2048]{2,1,0:T(8,128)(2,1)}) %all-gather.10.cloned.1.call-update) | async-done | bytes 4194320 | tf_op jit(solution)/shard_map/all_gather | solution.py:85
  369.5 3.0 convert_reduce_fusion.1
  374.2 3.0 convolution_convert_fusion.1
  377.5 4.2 convolution_convert_fusion.2
  382.2 5.0 convolution_convert_fusion.3
  387.2 2.2 reshape.170
  389.4 3.3 fusion.131
  392.7 2.5 fusion.54
  395.7 1.5 reshape.173
  397.4 24.8 %all_to_all.56 = bf16[256,8,256]{2,0,1:T(8,128)(2,1)S(1)} all-to-all(bf16[256,8,256]{2,0,1:T(8,128)(2,1)S(1)} %bitcast.138), channel_id=1, replica_groups=mesh['seq'=16,'head'=8] {'head'}, dimensions={1} | all-to-all | bytes 2097152 | tf_op jit(solution)/shard_map/all_to_all | solution.py:96
  422.2 74.8 %all-gather.12.cloned.1.call-done = bf16[16,64,2048]{2,1,0:T(8,128)(2,1)} async-done(((bf16[16,64,256]{2,1,0:T(8,128)(2,1)}), bf16[16,64,2048]{2,1,0:T(8,128)(2,1)}) %all-gather.12.cloned.1.call-update) | async-done | bytes 4194320 | tf_op jit(solution)/shard_map/all_gather | solution.py:97
  497.0 4.2 fusion.68
  501.3 100.4 %all-gather.14.cloned.1.call-done = bf16[16,64,2048]{2,1,0:T(8,128)(2,1)} async-done(((bf16[16,64,256]{2,1,0:T(8,128)(2,1)}), bf16[16,64,2048]{2,1,0:T(8,128)(2,1)}) %all-gather.14.cloned.1.call-update) | async-done | bytes 4194320 | tf_op jit(solution)/shard_map/all_gather | solution.py:101
  601.7 3.0 convert_reduce_fusion
  606.4 15.3 %fusion.45 = bf16[16,64,2048]{2,1,0:T(8,128)(2,1)} fusion(bf16[1024,2048]{1,0:T(8,128)(2,1)} %param.15, bf16[16,64,2048]{2,1,0:T(8,128)(2,1)} %all-gather.14.cloned.1.call-done, bf16[2048,1024]{1,0:T(8,128)(2,1)} %param.14, f32[2048]{0:T(1024)S(1)} %bitcast.152, f32[2048]{0:T(1024)S(1)} %bitcast.151, f32[16,64]{1,0:T(8,128)S(1)} %add_rsqrt_fusion, ...), kind=kOutput, calls=%fused_computation.54 | convolution fusion | flops 8614051840 | bytes 16801792 | tf_op jit(solution)/shard_map/dot_general | solution.py:105
  621.7 2.8 copy.89
  624.5 52.6 %all_to_all.57 = bf16[8,16,64,256]{3,2,1,0:T(8,128)(2,1)S(1)} all-to-all(bf16[8,16,64,256]{3,2,1,0:T(8,128)(2,1)S(1)} %bitcast.133), channel_id=1, replica_groups=mesh['seq'=16,'head'=8] {'head'}, dimensions={0} | all-to-all | bytes 8388608 | tf_op jit(solution)/shard_map/all_to_all | solution.py:17
  (52 shorter events, 16.3 us)
Async XLA Ops:
  6.5 101.0 %all-gather.6.cloned.1.call-start = ((), (), s32[]{:S(2)}) async-start(), calls=%async_computation.4 | async-start | bytes 4718592 | tf_op jit(solution)/shard_map/all_gather | solution.py:68
  7.3 241.3 %all-gather.8.cloned.1.call-start = ((), (), s32[]{:S(2)}) async-start(), calls=%async_computation.5 | async-start | bytes 4718592 | tf_op jit(solution)/shard_map/all_gather | solution.py:82
  107.6 3.4 copy-start
  112.3 1.9 copy-start.8
  131.4 16.0 %copy-start.5 = (bf16[256,2048]{1,0:T(8,128)(2,1)S(1)}, bf16[256,2048]{1,0:T(8,128)(2,1)}, u32[]{:S(2)}) copy-start(bf16[256,2048]{1,0:T(8,128)(2,1)} %param.11) | copy-start | bytes 3145732
  147.4 101.2 %copy-start.7 = (bf16[1,1024,256]{2,1,0:T(8,128)(2,1)S(1)}, bf16[1,1024,256]{2,1,0:T(8,128)(2,1)}, u32[]{:S(2)}) copy-start(bf16[1,1024,256]{2,1,0:T(8,128)(2,1)} %param.8) | copy-start | bytes 1572868
  148.7 28.2 %all-to-all-start = ((bf16[256,8,256]{0,2,1:T(8,128)(2,1)}), bf16[256,8,256]{0,2,1:T(8,128)(2,1)S(1)}, u32[]{:S(2)}, u32[]{:S(2)}) async-start(bf16[256,8,256]{0,2,1:T(8,128)(2,1)} %bitcast.14), calls=%async_computation | async-start | bytes 2097152 | tf_op jit(solution)/shard_map/all_to_all | solution.py:81
  154.7 214.7 %all-gather.10.cloned.1.call-start = ((), (), s32[]{:S(2)}) async-start(), calls=%async_computation.6 | async-start | bytes 4718592 | tf_op jit(solution)/shard_map/all_gather | solution.py:85
  274.7 222.4 %all-gather.12.cloned.1.call-start = ((), (), s32[]{:S(2)}) async-start(), calls=%async_computation.7 | async-start | bytes 4718592 | tf_op jit(solution)/shard_map/all_gather | solution.py:97
  369.5 3.4 copy-start.1
  395.2 2.1 copy-start.6
  395.2 101.8 %copy-start.3 = (bf16[1,1024,256]{2,1,0:T(8,128)(2,1)S(1)}, bf16[1,1024,256]{2,1,0:T(8,128)(2,1)}, u32[]{:S(2)}) copy-start(bf16[1,1024,256]{2,1,0:T(8,128)(2,1)} %copy.55) | copy-start | bytes 1572868
  397.2 204.5 %all-gather.14.cloned.1.call-start = ((), (), s32[]{:S(2)}) async-start(), calls=%async_computation.8 | async-start | bytes 4718592 | tf_op jit(solution)/shard_map/all_gather | solution.py:101
  601.7 3.4 copy-start.2
  677.1 1.0 copy-start.4
Sparse Core Ops, SparseCore 0:
  8.9 98.6 all-gather.5
  147.5 101.0 all-gather.7
  274.8 94.6 all-gather.9
  397.3 99.6 all-gather.11
  501.4 100.2 all-gather.13
where the time goes:
time: 696 us; the launch traced here: 686 us
  waiting for transfers between devices  462 us (66%)
  blocking collectives  93.3 us (13%)
  matrix products  74.2 us (11%)
  other arithmetic  21.1 us (3%)
  local copies, waits for them, and re-layouts  15.2 us (2%)
  between operations  13.6 us (2%)
    all_gather x1, waiting for transfers between devices, per_device(): full_two = lax.all_gather(stream_two, 'head', axis=2, tiled=True)  100 us
    all_gather x1, waiting for transfers between devices, per_device(): full_spatial = lax.all_gather(latent, 'head', axis=2, tiled=True)  99.1 us
    all_gather x1, waiting for transfers between devices, per_device(): full_temporal = lax.all_gather(stream_temporal, 'head', axis=2, tiled=True)  94.6 us
    all_gather x1, waiting for transfers between devices, per_device(): lax.all_gather(temporal, 'head', axis=2, tiled=True)  74.8 us
    all_gather x1, waiting for transfers between devices, per_device(): lax.all_gather(spatial, 'head', axis=2, tiled=True)  71.1 us
    all_to_all x1, blocking collectives, sum_at_owner(): lax.all_to_all(split_up(shard, dim, devices), axis, 0, 0, tiled=True)  52.6 us
    all_to_all x1, blocking collectives, per_device(): lax.all_to_all(temporal_out, 'head', split_axis=1, concat_axis=0, tiled=T...  24.8 us
    all_to_all x1, waiting for transfers between devices, per_device(): lax.all_to_all(spatial_out, 'head', split_axis=1, concat_axis=0, tiled=True)  21.3 us
  transfers between devices with their start and end apart: 6, of which 6 were waited for; matrix products, arithmetic and copies ran while one was open for 1% of the time, Pallas kernels for 0%

commit v1 on v0

--- a/solution.py
+++ b/solution.py
@@ -4,6 +4,11 @@
 from jax.sharding import PartitionSpec as P
 
 HD = 64
+
+
+def all_parts(x, name, along):
+    blocks = lax.all_gather(x, name)
+    return jnp.concatenate(blocks, axis=along)
 
 
 def split_up(shard, dim, devices):
@@ -79,7 +84,7 @@
     )
     spatial = spatial.reshape(frames_local, patches, width_local)
     columns = lax.all_to_all(spatial_out, "head", split_axis=1, concat_axis=0, tiled=True)
-    reduced = column_adder(columns, lax.all_gather(spatial, "head", axis=2, tiled=True))
+    reduced = column_adder(columns, all_parts(spatial, "head", 2))
     stream_one = (latent.astype(jnp.float32) + local_rows[2] * reduced).astype(jnp.bfloat16)
     stream_temporal = lax.all_to_all(stream_one, "seq", split_axis=1, concat_axis=0, tiled=True)
     full_temporal = lax.all_gather(stream_temporal, "head", axis=2, tiled=True)

time: 696 us -> 703 us (1.010)
  local copies, waits for them, and re-layouts: 15.2 us -> 23.1 us
where the time goes in v1:
time: 703 us; the launch traced here: 693 us
  waiting for transfers between devices  462 us (66%)
  blocking collectives  93.3 us (13%)
  matrix products  73.5 us (10%)
  local copies, waits for them, and re-layouts  23.1 us (3%)
  other arithmetic  21.1 us (3%)
  between operations  13.7 us (2%)
    all_gather x1, waiting for transfers between devices, per_device(): full_two = lax.all_gather(stream_two, 'head', axis=2, tiled=True)  100 us
    all_gather x1, waiting for transfers between devices, per_device(): full_spatial = lax.all_gather(latent, 'head', axis=2, tiled=True)  99.1 us
    all_gather x1, waiting for transfers between devices, per_device(): full_temporal = lax.all_gather(stream_temporal, 'head', axis=2, tiled=True)  94.6 us
    all_gather x1, waiting for transfers between devices, per_device(): lax.all_gather(temporal, 'head', axis=2, tiled=True)  74.8 us
    all_gather x1, waiting for transfers between devices, all_parts(): blocks = lax.all_gather(x, name)  71.1 us
    all_to_all x1, blocking collectives, sum_at_owner(): lax.all_to_all(split_up(shard, dim, devices), axis, 0, 0, tiled=True)  52.6 us
    all_to_all x1, blocking collectives, per_device(): lax.all_to_all(temporal_out, 'head', split_axis=1, concat_axis=0, tiled=T...  24.9 us
    all_to_all x1, waiting for transfers between devices, per_device(): lax.all_to_all(spatial_out, 'head', split_axis=1, concat_axis=0, tiled=True)  21.3 us
  transfers between devices with their start and end apart: 6, of which 6 were waited for; matrix products, arithmetic and copies ran while one was open for 1% of the time, Pallas kernels for 0%

profile of v1, /device:TPU:8, one launch (start us, length us, event | category | flops | bytes accessed | tf_op | source)
XLA Modules:
  0.0 692.6 jit_solution(3294920829588243222)
XLA Ops:
  8.4 99.1 %all-gather.6.cloned.1.call-done = bf16[1,1024,2048]{2,1,0:T(8,128)(2,1)} async-done(((bf16[1,1024,256]{2,1,0:T(8,128)(2,1)}), bf16[1,1024,2048]{2,1,0:T(8,128)(2,1)}) %all-gather.6.cloned.1.call-update) | async-done | bytes 4194320 | tf_op jit(solution)/shard_map/all_gather | solution.py:73
  107.6 3.0 convert_reduce_fusion.2
  112.3 1.9 fusion.33
  114.2 1.3 convolution_convert_fusion.6
  118.1 5.2 fusion.119
  123.3 8.1 %fusion.125 = f32[4,1024,1024]{1,2,0:T(8,128)} fusion(bf16[1024,4,64]{0,2,1:T(8,128)(2,1)S(1)} %bitcast.136, bf16[1024,4,64]{0,2,1:T(8,128)(2,1)S(1)} %bitcast.138), kind=kOutput, calls=%fused_computation.122 | convolution fusion | flops 536870912 | bytes 17825792 | tf_op jit(solution)/shard_map/while/body/eval_jaxpr/glhd,gmhd->ghlm/dot_general | solution.py:39
  131.4 15.3 %fusion.58 = bf16[4,64,1024]{2,1,0:T(8,128)(2,1)S(1)} fusion(bf16[1024,4,64]{0,2,1:T(8,128)(2,1)S(1)} %bitcast.156, f32[4,1024]{1,0:T(4,128)S(1)} %fusion.119, f32[4,1024,1024]{1,2,0:T(8,128)} %fusion.125), kind=kOutput, calls=%fused_computation.76 | convolution fusion | flops 558109696 | bytes 17842176 | tf_op jit(solution)/shard_map/while/body/eval_jaxpr/ghlm,gmhd->glhd/dot_general | solution.py:43
  147.7 1.8 copy.46
  149.5 5.5 all-to-all-start
  155.9 21.3 %all-to-all-done = bf16[256,8,256]{0,2,1:T(8,128)(2,1)S(1)} async-done(((bf16[256,8,256]{0,2,1:T(8,128)(2,1)}), bf16[256,8,256]{0,2,1:T(8,128)(2,1)S(1)}, u32[]{:S(2)}, u32[]{:S(2)}) %all-to-all-start) | async-done | bytes 1048608 | tf_op jit(solution)/shard_map/all_to_all | solution.py:86
  177.8 71.1 %all-gather.8.cloned.1.call-done = bf16[8,1,1024,256]{3,2,1,0:T(8,128)(2,1)} async-done(((bf16[1,1,1024,256]{3,2,1,0:T(8,128)(2,1)}), bf16[8,1,1024,256]{3,2,1,0:T(8,128)(2,1)}) %all-gather.8.cloned.1.call-update) | async-done | bytes 4194320 | tf_op jit(solution)/shard_map/all_gather | solution.py:10
  248.9 6.5 copy.45
  255.4 3.5 fusion.57
  260.2 3.8 reduce.6
  264.1 15.9 %all_to_all.55 = bf16[16,2,8192]{2,1,0:T(2,128)(2,1)S(1)} all-to-all(bf16[16,2,8192]{2,1,0:T(2,128)(2,1)S(1)} %reshape.183), channel_id=1, replica_groups=mesh['seq'=16,'head'=8] {'seq'}, dimensions={0} | all-to-all | bytes 1048576 | tf_op jit(solution)/shard_map/all_to_all | solution.py:89
  281.6 94.6 %all-gather.10.cloned.1.call-done = bf16[16,64,2048]{2,1,0:T(8,128)(2,1)} async-done(((bf16[16,64,256]{2,1,0:T(8,128)(2,1)}), bf16[16,64,2048]{2,1,0:T(8,128)(2,1)}) %all-gather.10.cloned.1.call-update) | async-done | bytes 4194320 | tf_op jit(solution)/shard_map/all_gather | solution.py:90
  376.2 3.0 convert_reduce_fusion.1
  380.9 3.0 convolution_convert_fusion.1
  384.3 4.2 convolution_convert_fusion.2
  388.9 5.0 convolution_convert_fusion.3
  393.9 2.2 reshape.172
  396.2 3.3 fusion.120
  399.5 2.5 fusion.52
  402.5 1.5 reshape.175
  404.1 24.9 %all_to_all.56 = bf16[256,8,256]{2,0,1:T(8,128)(2,1)S(1)} all-to-all(bf16[256,8,256]{2,0,1:T(8,128)(2,1)S(1)} %bitcast.132), channel_id=1, replica_groups=mesh['seq'=16,'head'=8] {'head'}, dimensions={1} | all-to-all | bytes 2097152 | tf_op jit(solution)/shard_map/all_to_all | solution.py:101
  429.0 74.8 %all-gather.12.cloned.1.call-done = bf16[16,64,2048]{2,1,0:T(8,128)(2,1)} async-done(((bf16[16,64,256]{2,1,0:T(8,128)(2,1)}), bf16[16,64,2048]{2,1,0:T(8,128)(2,1)}) %all-gather.12.cloned.1.call-update) | async-done | bytes 4194320 | tf_op jit(solution)/shard_map/all_gather | solution.py:102
  503.8 4.2 fusion.56
  508.1 100.4 %all-gather.14.cloned.1.call-done = bf16[16,64,2048]{2,1,0:T(8,128)(2,1)} async-done(((bf16[16,64,256]{2,1,0:T(8,128)(2,1)}), bf16[16,64,2048]{2,1,0:T(8,128)(2,1)}) %all-gather.14.cloned.1.call-update) | async-done | bytes 4194320 | tf_op jit(solution)/shard_map/all_gather | solution.py:106
  608.5 3.0 convert_reduce_fusion
  613.2 15.3 %fusion.43 = bf16[16,64,2048]{2,1,0:T(8,128)(2,1)} fusion(bf16[1024,2048]{1,0:T(8,128)(2,1)} %param.15, bf16[16,64,2048]{2,1,0:T(8,128)(2,1)} %all-gather.14.cloned.1.call-done, bf16[2048,1024]{1,0:T(8,128)(2,1)} %param.14, f32[2048]{0:T(1024)S(1)} %bitcast.146, f32[2048]{0:T(1024)S(1)} %bitcast.145, f32[16,64]{1,0:T(8,128)S(1)} %add_rsqrt_fusion, ...), kind=kOutput, calls=%fused_computation.52 | convolution fusion | flops 8614051840 | bytes 16801792 | tf_op jit(solution)/shard_map/dot_general | solution.py:110
  628.5 2.8 copy.92
  631.2 52.6 %all_to_all.57 = bf16[8,16,64,256]{3,2,1,0:T(8,128)(2,1)S(1)} all-to-all(bf16[8,16,64,256]{3,2,1,0:T(8,128)(2,1)S(1)} %bitcast.126), channel_id=1, replica_groups=mesh['seq'=16,'head'=8] {'head'}, dimensions={0} | all-to-all | bytes 8388608 | tf_op jit(solution)/shard_map/all_to_all | solution.py:22
  (54 shorter events, 18.6 us)
Async XLA Ops:
  6.5 101.0 %all-gather.6.cloned.1.call-start = ((), (), s32[]{:S(2)}) async-start(), calls=%async_computation.4 | async-start | bytes 4718592 | tf_op jit(solution)/shard_map/all_gather | solution.py:73
  7.3 241.6 %all-gather.8.cloned.1.call-start = ((), (), s32[]{:S(2)}) async-start(), calls=%async_computation.5 | async-start | bytes 4718592 | tf_op jit(solution)/shard_map/all_gather | solution.py:10
  107.6 3.4 copy-start
  112.3 1.9 copy-start.8
  131.4 16.3 %copy-start.5 = (bf16[256,2048]{1,0:T(8,128)(2,1)S(1)}, bf16[256,2048]{1,0:T(8,128)(2,1)}, u32[]{:S(2)}) copy-start(bf16[256,2048]{1,0:T(8,128)(2,1)} %param.11) | copy-start | bytes 3145732
  149.5 27.7 %all-to-all-start = ((bf16[256,8,256]{0,2,1:T(8,128)(2,1)}), bf16[256,8,256]{0,2,1:T(8,128)(2,1)S(1)}, u32[]{:S(2)}, u32[]{:S(2)}) async-start(bf16[256,8,256]{0,2,1:T(8,128)(2,1)} %bitcast.15), calls=%async_computation | async-start | bytes 2097152 | tf_op jit(solution)/shard_map/all_to_all | solution.py:86
  155.0 221.2 %all-gather.10.cloned.1.call-start = ((), (), s32[]{:S(2)}) async-start(), calls=%async_computation.6 | async-start | bytes 4718592 | tf_op jit(solution)/shard_map/all_gather | solution.py:90
  177.8 77.6 %copy-start.7 = (bf16[1,1024,256]{2,1,0:T(8,128)(2,1)S(1)}, bf16[1,1024,256]{2,1,0:T(8,128)(2,1)}, u32[]{:S(2)}) copy-start(bf16[1,1024,256]{2,1,0:T(8,128)(2,1)} %param.8) | copy-start | bytes 1572868
  281.4 222.4 %all-gather.12.cloned.1.call-start = ((), (), s32[]{:S(2)}) async-start(), calls=%async_computation.7 | async-start | bytes 4718592 | tf_op jit(solution)/shard_map/all_gather | solution.py:102
  376.2 3.4 copy-start.1
  402.0 2.1 copy-start.6
  402.0 101.8 %copy-start.3 = (bf16[1,1024,256]{2,1,0:T(8,128)(2,1)S(1)}, bf16[1,1024,256]{2,1,0:T(8,128)(2,1)}, u32[]{:S(2)}) copy-start(bf16[1,1024,256]{2,1,0:T(8,128)(2,1)} %copy.58) | copy-start | bytes 1572868
  404.0 204.5 %all-gather.14.cloned.1.call-start = ((), (), s32[]{:S(2)}) async-start(), calls=%async_computation.8 | async-start | bytes 4718592 | tf_op jit(solution)/shard_map/all_gather | solution.py:106
  608.5 3.4 copy-start.2
  683.8 1.0 copy-start.4
Sparse Core Ops, SparseCore 0:
  8.9 98.6 all-gather.5
  147.8 101.0 all-gather.7
  281.5 94.6 all-gather.9
  404.1 99.6 all-gather.11
  508.2 100.2 all-gather.13
